TPU v7x, 256 devices: a whole 4x4x8 slice. The times are simulated.
256 devices in a mesh: gx: 8 (over z), gy: 8 (over y, x_hi), gz: 4 (over x_lo, core).
Axes of the slice: x: 4 (x_hi: 2, x_lo: 2; x = x_hi * 2 + x_lo), y: 4, z: 8, core: 2. Of those that a mesh axis runs over, the one named last changes fastest.
Arguments:
- hidden_acts: bfloat16 [4, 8, 8, 256, 16384], P('gz', 'gy', 'gx'), may hold values from -6 to 6
- output_grad: bfloat16 [4, 8, 8, 256, 32], P('gz', 'gy', 'gx'), may hold values from -6 to 6
- weights: bfloat16 [4, 8, 8, 32, 16384], P('gz', 'gy', 'gx'), may hold values from -6 to 6
- momentum: bfloat16 [4, 8, 8, 32, 16384], P('gz', 'gy', 'gx'), may hold values from -48 to 48
- worker_of_slot: int32 [256], replicated, may hold values from 0 to 255, each once
- round_shift: int32 [8], replicated, may hold values from 0 to 7, as said below
Outputs:
- mixed: bfloat16 [8, 8, 4, 32, 16384], P('gx', 'gy', 'gz')
- new_momentum: bfloat16 [4, 8, 8, 32, 16384], P('gz', 'gy', 'gx')
Inputs may be any that keep to these rules, and one draw needn't show every extreme that they name: `round_shift`: each entry is below log2 of 256, so offsets are powers of two below 256; some round has offset 256 / 2 and some round offset 1.
All inputs are finite; a program needn't handle non-finite values.
Results may differ from a plain program's by a relative error of at most 0.0081.
Values may be sent and summed in bfloat16 or wider, within the bound.
No kernel may reach another device: no remote copies, remote signals or barrier semaphores. Data moves between devices by JAX's collectives and lax.ppermute only.
A program may use at most 64 MiB of HBM per device.

v0:
```python
import jax
import jax.numpy as jnp
from jax import lax
from jax.experimental import pallas as pl
from jax.experimental.pallas import tpu as pltpu
from jax.sharding import PartitionSpec as P


BLOCK = 8192
SUB = 8

learn_rate = 0.01
beta_keep = 0.9


def velocity_of(grad_out_ref, first_ref, second_ref, moment_ref):
    tokens = first_ref.shape[0]
    grad = jnp.dot(
        grad_out_ref[:, :tokens], first_ref[...], preferred_element_type=jnp.float32
    ) + jnp.dot(grad_out_ref[:, tokens:], second_ref[...], preferred_element_type=jnp.float32)
    return beta_keep * moment_ref[...].astype(jnp.float32) + grad


def step_kernel(grad_out_ref, first_ref, second_ref, weight_ref, moment_ref, pieces_ref):
    velocity = velocity_of(grad_out_ref, first_ref, second_ref, moment_ref)
    stepped = (weight_ref[...].astype(jnp.float32) - learn_rate * velocity).astype(jnp.bfloat16)
    groups, count, _, width = pieces_ref.shape
    for group in range(groups):
        for at in range(count):
            pieces_ref[group, at] = stepped[
                group * SUB : (group + 1) * SUB, at * width : (at + 1) * width
            ]


def moment_kernel(grad_out_ref, first_ref, second_ref, moment_ref, new_moment_ref):
    velocity = velocity_of(grad_out_ref, first_ref, second_ref, moment_ref)
    new_moment_ref[...] = velocity.astype(jnp.bfloat16)


def in_hbm(*operands):
    return [pltpu.with_memory_space_constraint(a, pltpu.HBM) for a in operands]


def local_step(grad_out, hidden, weight, moment, workers):
    rows, cols = weight.shape
    tokens = hidden.shape[0]
    groups = rows // SUB
    width = cols * groups // workers
    block = pl.BlockSpec((rows, BLOCK), lambda i: (0, i))
    return pl.pallas_call(
        step_kernel,
        grid=(cols // BLOCK,),
        in_specs=[
            pl.BlockSpec((rows, tokens), lambda i: (0, 0)),
            pl.BlockSpec((tokens // 2, BLOCK), lambda i: (0, i)),
            pl.BlockSpec((tokens // 2, BLOCK), lambda i: (1, i)),
            block,
            block,
        ],
        out_specs=pl.BlockSpec((groups, BLOCK // width, SUB, width), lambda i: (0, i, 0, 0)),
        out_shape=jax.ShapeDtypeStruct((groups, cols // width, SUB, width), jnp.bfloat16),
        compiler_params=pltpu.CompilerParams(vmem_limit_bytes=24 << 20),
        name="local_step",
    )(*in_hbm(grad_out, hidden, hidden, weight, moment))


def momentum_step(grad_out, hidden, moment):
    rows, cols = moment.shape
    tokens = hidden.shape[0]
    block = pl.BlockSpec((rows, BLOCK), lambda i: (0, i))
    return pl.pallas_call(
        moment_kernel,
        grid=(cols // BLOCK,),
        in_specs=[
            pl.BlockSpec((rows, tokens), lambda i: (0, 0)),
            pl.BlockSpec((tokens // 2, BLOCK), lambda i: (0, i)),
            pl.BlockSpec((tokens // 2, BLOCK), lambda i: (1, i)),
            block,
        ],
        out_specs=block,
        out_shape=jax.ShapeDtypeStruct((rows, cols), jnp.bfloat16),
        compiler_params=pltpu.CompilerParams(vmem_limit_bytes=24 << 20),
        name="momentum_step",
    )(*in_hbm(grad_out, hidden, hidden, moment))


def mixing_kernel(shift_ref, worker_ref, out_ref):
    workers = worker_ref.shape[1]
    half = workers // 2
    row = lax.broadcasted_iota(jnp.int32, (workers, workers), 0)
    col = lax.broadcasted_iota(jnp.int32, (workers, workers), 1)
    gap = (row - col) & (workers - 1)
    mix = (row == worker_ref[...]).astype(jnp.float32)
    for step in range(shift_ref.shape[0]):
        offset = jnp.left_shift(jnp.int32(1), shift_ref[step])
        one = ((gap == 0) | (gap == offset)).astype(jnp.bfloat16)
        mix = jnp.dot(one, mix.astype(jnp.bfloat16), preferred_element_type=jnp.float32)
    mix = mix[:half].astype(jnp.bfloat16)
    wide = workers * SUB
    spread_col = (
        lax.broadcasted_iota(jnp.int32, (workers, wide), 1) // SUB
        == lax.broadcasted_iota(jnp.int32, (workers, wide), 0)
    ).astype(jnp.bfloat16)
    wide_mix = jnp.dot(mix, spread_col, preferred_element_type=jnp.float32)
    out_ref[...] = wide_mix * (1.0 / workers)


def mixing(round_shift, held):
    workers = held.shape[1]
    return pl.pallas_call(
        mixing_kernel,
        in_specs=[
            pl.BlockSpec(memory_space=pltpu.SMEM),
            pl.BlockSpec(memory_space=pltpu.VMEM),
        ],
        out_specs=pl.BlockSpec(memory_space=pltpu.VMEM),
        out_shape=pltpu.VMEM((workers // 2, workers * SUB), jnp.float32),
        compiler_params=pltpu.CompilerParams(vmem_limit_bytes=24 << 20),
        name="mixing",
    )(round_shift, held)


def mix_kernel(mix_ref, rows_ref, out_ref, full_ref):
    half, wide = mix_ref.shape
    same = (
        lax.broadcasted_iota(jnp.int32, (SUB, wide), 1) & (SUB - 1)
        == lax.broadcasted_iota(jnp.int32, (SUB, wide), 0)
    )
    for at in range(0, half, 2):
        lines = [
            jnp.where(same, jnp.broadcast_to(mix_ref[k : k + 1], (SUB, wide)), 0.0)
            for k in (at, at + 1)
        ]
        full_ref[at * SUB : (at + 2) * SUB] = jnp.concatenate(lines, axis=0).astype(jnp.bfloat16)
    mixed = jnp.dot(full_ref[...], rows_ref[...], preferred_element_type=jnp.float32)
    mixed = mixed.astype(jnp.bfloat16)
    out_ref[: half * SUB] = mixed
    out_ref[half * SUB :] = mixed


def mix(matrix, rows):
    half, wide = matrix.shape
    return pl.pallas_call(
        mix_kernel,
        in_specs=[
            pl.BlockSpec(memory_space=pltpu.VMEM),
            pl.BlockSpec(memory_space=pltpu.VMEM),
        ],
        out_specs=pl.BlockSpec(memory_space=pltpu.VMEM),
        out_shape=pltpu.VMEM(rows.shape, jnp.bfloat16),
        scratch_shapes=[pltpu.VMEM((half * SUB, wide), jnp.bfloat16)],
        compiler_params=pltpu.CompilerParams(vmem_limit_bytes=24 << 20),
        name="mix",
    )(
        pltpu.with_memory_space_constraint(matrix, pltpu.VMEM),
        pltpu.with_memory_space_constraint(rows, pltpu.VMEM),
    )


def exchange(pieces):
    return lax.all_to_all(pieces, ("gx", "gy", "gz"), split_axis=0, concat_axis=0, tiled=True)


def shards(hidden_acts, output_grad, weights, momentum, worker_of_slot, round_shift):
    hidden = hidden_acts.reshape(hidden_acts.shape[-2:])
    grad_out = output_grad.reshape(output_grad.shape[-2:]).T
    weight = weights.reshape(weights.shape[-2:])
    moment = momentum.reshape(momentum.shape[-2:])
    count_x = lax.axis_size("gx")
    count_y = lax.axis_size("gy")
    count_z = lax.axis_size("gz")
    workers = count_x * count_y * count_z
    rows, _ = weight.shape
    groups = rows // SUB
    held = worker_of_slot.reshape(count_z, count_y, count_x).transpose(2, 1, 0)
    matrix = mixing(round_shift, held.reshape(1, workers))
    pieces = local_step(grad_out, hidden, weight, moment, workers)
    received = exchange(pieces.reshape(workers, SUB, -1))
    new_moment = momentum_step(grad_out, hidden, moment)
    width = received.shape[-1]
    mixed = mix(matrix, received.reshape(workers * SUB, width))
    returned = exchange(mixed.reshape(workers, SUB, width))
    block = returned.reshape(groups, workers // groups, SUB, width).transpose(0, 2, 1, 3)
    return (block.reshape(weights.shape), new_moment.reshape(momentum.shape))


def solution(mesh):
    placed = (
        P("gz", "gy", "gx", None, None),
        P("gz", "gy", "gx", None, None),
        P("gz", "gy", "gx", None, None),
        P("gz", "gy", "gx", None, None),
        P(),
        P(),
    )
    return jax.shard_map(
        shards,
        mesh=mesh,
        in_specs=placed,
        out_specs=(P("gx", "gy", "gz", None, None), P("gz", "gy", "gx", None, None)),
        check_vma=False,
    )
```

profile of v0, /device:TPU:1, one launch (start us, length us, event | category | flops | bytes accessed | tf_op | source)
XLA Modules:
  0.0 92.3 jit_solution(12758170308764605886)
XLA Ops:
  0.6 0.0 copy-start.1
  0.6 0.0 copy-start
  0.7 5.5 %local_step.1 = bf16[4,64,8,256]{3,2,1,0:T(8,128)(2,1)} custom-call(bf16[32,256]{1,0:T(8,128)(2,1)} %bitcast.27, bf16[256,16384]{1,0:T(8,128)(2,1)} %bitcast.17, bf16[256,16384]{1,0:T(8,128)(2,1)} %bitcast.18, bf16[32,16384]{1,0:T(8,128)(2,1)} %bitcast.24, bf16[32,16384]{1,0:T(8,128)(2,1)} %bitcast.22), custom_call_target="tpu_custom_call" | custom-call | tf_op jit(solution)/shard_map/local_step/pallas_call | solution.py:50
  6.2 15.6 %all-to-all-start = ((bf16[256,8,256]{2,1,0:T(8,128)(2,1)}), bf16[256,8,256]{2,1,0:T(8,128)(2,1)S(1)}, u32[]{:S(2)}, u32[]{:S(2)}) async-start(bf16[256,8,256]{2,1,0:T(8,128)(2,1)} %bitcast.6), calls=%async_computation | async-start | bytes 2097152 | tf_op jit(solution)/shard_map/all_to_all | solution.py:161
  21.8 0.0 copy-done.1
  21.8 0.1 reshape.40
  21.9 0.1 copy.8
  22.0 0.1 reshape.41.worker_ref
  22.1 0.0 copy-done
  22.2 2.3 %mixing.1.mix_ref = f32[128,2048]{1,0:T(8,128)S(1)} custom-call(s32[8]{0:T(128)S(1)} %copy-done, s32[1,256]{1,0:T(1,128)S(1)} %reshape.41.worker_ref), custom_call_target="tpu_custom_call" | custom-call | tf_op jit(solution)/shard_map/mixing/pallas_call | solution.py:110
  24.4 27.9 %all-to-all-done = bf16[256,8,256]{2,1,0:T(8,128)(2,1)S(1)} async-done(((bf16[256,8,256]{2,1,0:T(8,128)(2,1)}), bf16[256,8,256]{2,1,0:T(8,128)(2,1)S(1)}, u32[]{:S(2)}, u32[]{:S(2)}) %all-to-all-start) | async-done | bytes 1048608 | tf_op jit(solution)/shard_map/all_to_all | solution.py:161
  52.4 2.2 %mix.1 = bf16[2048,256]{1,0:T(8,128)(2,1)} custom-call(f32[128,2048]{1,0:T(8,128)S(1)} %mixing.1.mix_ref, bf16[2048,256]{1,0:T(8,128)(2,1)S(1)} %bitcast.16), custom_call_target="tpu_custom_call" | custom-call | tf_op jit(solution)/shard_map/mix/pallas_call | solution.py:143
  54.6 6.4 %all-to-all-start.1 = ((bf16[256,8,256]{2,1,0:T(8,128)(2,1)}), bf16[256,8,256]{2,1,0:T(8,128)(2,1)S(1)}, u32[]{:S(2)}, u32[]{:S(2)}) async-start(bf16[256,8,256]{2,1,0:T(8,128)(2,1)} %bitcast.8), calls=%async_computation.1 | async-start | bytes 2097152 | tf_op jit(solution)/shard_map/all_to_all | solution.py:161
  61.0 5.2 %momentum_step.1 = bf16[32,16384]{1,0:T(8,128)(2,1)} custom-call(bf16[32,256]{1,0:T(8,128)(2,1)} %bitcast.28, bf16[256,16384]{1,0:T(8,128)(2,1)} %bitcast.19, bf16[256,16384]{1,0:T(8,128)(2,1)} %bitcast.20, bf16[32,16384]{1,0:T(8,128)(2,1)} %bitcast.23), custom_call_target="tpu_custom_call" | custom-call | tf_op jit(solution)/shard_map/momentum_step/pallas_call | solution.py:71
  66.2 25.1 %all-to-all-done.1 = bf16[256,8,256]{2,1,0:T(8,128)(2,1)S(1)} async-done(((bf16[256,8,256]{2,1,0:T(8,128)(2,1)}), bf16[256,8,256]{2,1,0:T(8,128)(2,1)S(1)}, u32[]{:S(2)}, u32[]{:S(2)}) %all-to-all-start.1) | async-done | bytes 1048608 | tf_op jit(solution)/shard_map/all_to_all | solution.py:161
  91.3 1.0 %copy.10 = bf16[1,1,1,32,16384]{4,3,2,1,0:T(8,128)(2,1)} copy(bf16[1,1,1,32,16384]{4,3,2,1,0:T(8,128)(2,1)S(1)} %bitcast.21) | data formatting | bytes 2097152
Async XLA Ops:
  0.6 21.2 %copy-start.1 = (s32[256]{0:T(256)S(1)}, s32[256]{0:T(256)}, u32[]{:S(2)}) copy-start(s32[256]{0:T(256)} %param.10) | copy-start | bytes 3076
  0.6 21.5 %copy-start = (s32[8]{0:T(128)S(1)}, s32[8]{0:T(128)}, u32[]{:S(2)}) copy-start(s32[8]{0:T(128)} %shift_ref.1) | copy-start | bytes 100
  6.2 46.2 %all-to-all-start = ((bf16[256,8,256]{2,1,0:T(8,128)(2,1)}), bf16[256,8,256]{2,1,0:T(8,128)(2,1)S(1)}, u32[]{:S(2)}, u32[]{:S(2)}) async-start(bf16[256,8,256]{2,1,0:T(8,128)(2,1)} %bitcast.6), calls=%async_computation | async-start | bytes 2097152 | tf_op jit(solution)/shard_map/all_to_all | solution.py:161
  54.6 36.7 %all-to-all-start.1 = ((bf16[256,8,256]{2,1,0:T(8,128)(2,1)}), bf16[256,8,256]{2,1,0:T(8,128)(2,1)S(1)}, u32[]{:S(2)}, u32[]{:S(2)}) async-start(bf16[256,8,256]{2,1,0:T(8,128)(2,1)} %bitcast.8), calls=%async_computation.1 | async-start | bytes 2097152 | tf_op jit(solution)/shard_map/all_to_all | solution.py:161
where the time goes:
time: 92.6 us; the launch traced here: 92.3 us
  waiting for transfers between devices  53.1 us (57%)
  starting transfers between devices  22.1 us (24%)
  Pallas kernels  15.2 us (16%)
  local copies, waits for them, and re-layouts  1.31 us (1%)
    all_to_all x2, waiting for transfers between devices, exchange(): lax.all_to_all(pieces, ('gx', 'gy', 'gz'), split_axis=0, concat_axis=0, t...  53.1 us
    all_to_all x2, starting transfers between devices, exchange(): lax.all_to_all(pieces, ('gx', 'gy', 'gz'), split_axis=0, concat_axis=0, t...  22.1 us
    pallas_call x1, Pallas kernels, local_step(): pl.pallas_call(step_kernel, grid=(cols // BLOCK,), in_specs=[pl.BlockSpec...  5.5 us
    pallas_call x1, Pallas kernels, momentum_step(): pl.pallas_call(moment_kernel, grid=(cols // BLOCK,), in_specs=[pl.BlockSp...  5.17 us
    pallas_call x1, Pallas kernels, mixing(): pl.pallas_call(mixing_kernel, in_specs=[pl.BlockSpec(memory_space=pltpu.S...  2.26 us
    pallas_call x1, Pallas kernels, mix(): pl.pallas_call(mix_kernel, in_specs=[pl.BlockSpec(memory_space=pltpu.VMEM...  2.23 us
  transfers between devices with their start and end apart: 2, of which 2 were waited for; matrix products, arithmetic and copies ran while one was open for 0% of the time, Pallas kernels for 8%

commit v1 on v0

--- a/solution.py
+++ b/solution.py
@@ -1,3 +1,5 @@
+import functools
+
 import jax
 import jax.numpy as jnp
 from jax import lax
@@ -84,81 +86,97 @@
     )(*in_hbm(grad_out, hidden, hidden, moment))
 
 
-def mixing_kernel(shift_ref, worker_ref, out_ref):
-    workers = worker_ref.shape[1]
-    half = workers // 2
-    row = lax.broadcasted_iota(jnp.int32, (workers, workers), 0)
-    col = lax.broadcasted_iota(jnp.int32, (workers, workers), 1)
-    gap = (row - col) & (workers - 1)
-    mix = (row == worker_ref[...]).astype(jnp.float32)
+def mixing_kernel(sizes, shift_ref, out_ref):
+    _, count_y, count_z = sizes
+    half = out_ref.shape[0]
+    row = lax.broadcasted_iota(jnp.int32, (half, half), 0)
+    col = lax.broadcasted_iota(jnp.int32, (half, half), 1)
+    gap = (row - col) & (half - 1)
+    place_x = row // (count_y * count_z)
+    place_z = row // count_y % count_z
+    place_y = row % count_y
+    mix = ((place_x * count_y + place_y) * count_z + place_z == col).astype(jnp.float32)
     for step in range(shift_ref.shape[0]):
-        offset = jnp.left_shift(jnp.int32(1), shift_ref[step])
-        one = ((gap == 0) | (gap == offset)).astype(jnp.bfloat16)
-        mix = jnp.dot(one, mix.astype(jnp.bfloat16), preferred_element_type=jnp.float32)
-    mix = mix[:half].astype(jnp.bfloat16)
-    wide = workers * SUB
+        offset = jnp.left_shift(jnp.int32(1), shift_ref[step]) & (half - 1)
+        one = (gap == 0).astype(jnp.float32) + (gap == offset).astype(jnp.float32)
+        mix = jnp.dot(
+            mix.astype(jnp.bfloat16), one.astype(jnp.bfloat16), preferred_element_type=jnp.float32
+        )
+    wide = half * SUB
     spread_col = (
-        lax.broadcasted_iota(jnp.int32, (workers, wide), 1) // SUB
-        == lax.broadcasted_iota(jnp.int32, (workers, wide), 0)
+        lax.broadcasted_iota(jnp.int32, (half, wide), 1) // SUB
+        == lax.broadcasted_iota(jnp.int32, (half, wide), 0)
     ).astype(jnp.bfloat16)
-    wide_mix = jnp.dot(mix, spread_col, preferred_element_type=jnp.float32)
-    out_ref[...] = wide_mix * (1.0 / workers)
-
-
-def mixing(round_shift, held):
-    workers = held.shape[1]
-    return pl.pallas_call(
-        mixing_kernel,
-        in_specs=[
-            pl.BlockSpec(memory_space=pltpu.SMEM),
-            pl.BlockSpec(memory_space=pltpu.VMEM),
-        ],
+    wide_mix = jnp.dot(mix.astype(jnp.bfloat16), spread_col, preferred_element_type=jnp.float32)
+    out_ref[...] = wide_mix * (0.5 / half)
+
+
+def mixing(round_shift, sizes):
+    half = sizes[0] * sizes[1] * sizes[2] // 2
+    return pl.pallas_call(
+        functools.partial(mixing_kernel, sizes),
+        in_specs=[pl.BlockSpec(memory_space=pltpu.SMEM)],
         out_specs=pl.BlockSpec(memory_space=pltpu.VMEM),
-        out_shape=pltpu.VMEM((workers // 2, workers * SUB), jnp.float32),
+        out_shape=pltpu.VMEM((half, half * SUB), jnp.float32),
         compiler_params=pltpu.CompilerParams(vmem_limit_bytes=24 << 20),
         name="mixing",
-    )(round_shift, held)
-
-
-def mix_kernel(mix_ref, rows_ref, out_ref, full_ref):
+    )(round_shift)
+
+
+def mix_kernel(place_ref, mix_ref, rows_ref, out_ref, full_ref, pair_ref):
     half, wide = mix_ref.shape
     same = (
         lax.broadcasted_iota(jnp.int32, (SUB, wide), 1) & (SUB - 1)
         == lax.broadcasted_iota(jnp.int32, (SUB, wide), 0)
     )
     for at in range(0, half, 2):
+        pairs = [
+            (
+                rows_ref[place_ref[k]].astype(jnp.float32)
+                + rows_ref[place_ref[k + half]].astype(jnp.float32)
+            )
+            * 0.5
+            for k in (at, at + 1)
+        ]
+        pair_ref[at * SUB : (at + 2) * SUB] = jnp.concatenate(pairs, axis=0).astype(jnp.bfloat16)
         lines = [
             jnp.where(same, jnp.broadcast_to(mix_ref[k : k + 1], (SUB, wide)), 0.0)
             for k in (at, at + 1)
         ]
         full_ref[at * SUB : (at + 2) * SUB] = jnp.concatenate(lines, axis=0).astype(jnp.bfloat16)
-    mixed = jnp.dot(full_ref[...], rows_ref[...], preferred_element_type=jnp.float32)
+    mixed = jnp.dot(full_ref[...], pair_ref[...], preferred_element_type=jnp.float32)
     mixed = mixed.astype(jnp.bfloat16)
-    out_ref[: half * SUB] = mixed
-    out_ref[half * SUB :] = mixed
-
-
-def mix(matrix, rows):
-    half, wide = matrix.shape
+    out_ref[:wide] = mixed
+    out_ref[wide:] = mixed
+
+
+def mix(places, matrix, rows):
+    _, wide = matrix.shape
+    width = rows.shape[-1]
     return pl.pallas_call(
         mix_kernel,
         in_specs=[
+            pl.BlockSpec(memory_space=pltpu.SMEM),
             pl.BlockSpec(memory_space=pltpu.VMEM),
             pl.BlockSpec(memory_space=pltpu.VMEM),
         ],
         out_specs=pl.BlockSpec(memory_space=pltpu.VMEM),
-        out_shape=pltpu.VMEM(rows.shape, jnp.bfloat16),
-        scratch_shapes=[pltpu.VMEM((half * SUB, wide), jnp.bfloat16)],
+        out_shape=pltpu.VMEM((2 * wide, width), jnp.bfloat16),
+        scratch_shapes=[
+            pltpu.VMEM((wide, wide), jnp.bfloat16),
+            pltpu.VMEM((wide, width), jnp.bfloat16),
+        ],
         compiler_params=pltpu.CompilerParams(vmem_limit_bytes=24 << 20),
         name="mix",
     )(
+        places,
         pltpu.with_memory_space_constraint(matrix, pltpu.VMEM),
         pltpu.with_memory_space_constraint(rows, pltpu.VMEM),
     )
 
 
 def exchange(pieces):
-    return lax.all_to_all(pieces, ("gx", "gy", "gz"), split_axis=0, concat_axis=0, tiled=True)
+    return lax.all_to_all(pieces, ("gx", "gz", "gy"), split_axis=0, concat_axis=0, tiled=True)
 
 
 def shards(hidden_acts, output_grad, weights, momentum, worker_of_slot, round_shift):
@@ -172,13 +190,15 @@
     workers = count_x * count_y * count_z
     rows, _ = weight.shape
     groups = rows // SUB
-    held = worker_of_slot.reshape(count_z, count_y, count_x).transpose(2, 1, 0)
-    matrix = mixing(round_shift, held.reshape(1, workers))
+    held = worker_of_slot.reshape(count_z, count_y, count_x).transpose(2, 0, 1).reshape(1, workers)
+    order = jnp.arange(workers, dtype=jnp.int32)
+    places = jnp.sum(jnp.where(held == order[:, None], order[None, :], 0), axis=1, dtype=jnp.int32)
+    matrix = mixing(round_shift, (count_x, count_y, count_z))
     pieces = local_step(grad_out, hidden, weight, moment, workers)
     received = exchange(pieces.reshape(workers, SUB, -1))
     new_moment = momentum_step(grad_out, hidden, moment)
     width = received.shape[-1]
-    mixed = mix(matrix, received.reshape(workers * SUB, width))
+    mixed = mix(places, matrix, received)
     returned = exchange(mixed.reshape(workers, SUB, width))
     block = returned.reshape(groups, workers // groups, SUB, width).transpose(0, 2, 1, 3)
     return (block.reshape(weights.shape), new_moment.reshape(momentum.shape))

time: 92.6 us -> 93.9 us (1.014)
  waiting for transfers between devices: 53.1 us -> 54.9 us
    all_to_all x2, waiting for transfers between devices: 53.1 us -> 54.9 us  [exchange(): lax.all_to_all(pieces, ('gx', 'gz', 'gy'), split_axis=0, concat_axis=0, t...]
  transfers between devices with their start and end apart: 2 -> 2, of which waited for: 2 -> 2; matrix products, arithmetic and copies ran while one was open for 0% -> 0% of each run, Pallas kernels for 8% -> 7%
where the time goes in v1:
time: 93.9 us; the launch traced here: 93.7 us
  waiting for transfers between devices  54.9 us (58%)
  starting transfers between devices  22.1 us (24%)
  Pallas kernels  14.7 us (16%)
  local copies, waits for them, and re-layouts  1.24 us (1%)
    all_to_all x2, waiting for transfers between devices, exchange(): lax.all_to_all(pieces, ('gx', 'gz', 'gy'), split_axis=0, concat_axis=0, t...  54.9 us
    all_to_all x2, starting transfers between devices, exchange(): lax.all_to_all(pieces, ('gx', 'gz', 'gy'), split_axis=0, concat_axis=0, t...  22.1 us
    pallas_call x1, Pallas kernels, local_step(): pl.pallas_call(step_kernel, grid=(cols // BLOCK,), in_specs=[pl.BlockSpec...  5.5 us
    pallas_call x1, Pallas kernels, momentum_step(): pl.pallas_call(moment_kernel, grid=(cols // BLOCK,), in_specs=[pl.BlockSp...  5.17 us
    pallas_call x1, Pallas kernels, mix(): pl.pallas_call(mix_kernel, in_specs=[pl.BlockSpec(memory_space=pltpu.SMEM...  2.32 us
  transfers between devices with their start and end apart: 2, of which 2 were waited for; matrix products, arithmetic and copies ran while one was open for 0% of the time, Pallas kernels for 7%

profile of v1, /device:TPU:1, one launch (start us, length us, event | category | flops | bytes accessed | tf_op | source)
XLA Modules:
  0.0 93.7 jit_solution(4493026232061620795)
XLA Ops:
  0.6 0.0 copy-start
  0.6 0.0 copy-start.1
  0.7 5.5 %local_step.1 = bf16[4,64,8,256]{3,2,1,0:T(8,128)(2,1)} custom-call(bf16[32,256]{1,0:T(8,128)(2,1)} %bitcast.25, bf16[256,16384]{1,0:T(8,128)(2,1)} %bitcast.15, bf16[256,16384]{1,0:T(8,128)(2,1)} %bitcast.16, bf16[32,16384]{1,0:T(8,128)(2,1)} %bitcast.22, bf16[32,16384]{1,0:T(8,128)(2,1)} %bitcast.20), custom_call_target="tpu_custom_call" | custom-call | tf_op jit(solution)/shard_map/local_step/pallas_call | solution.py:52
  6.2 15.6 %all-to-all-start = ((bf16[256,8,256]{2,1,0:T(8,128)(2,1)}), bf16[256,8,256]{2,1,0:T(8,128)(2,1)S(1)}, u32[]{:S(2)}, u32[]{:S(2)}) async-start(bf16[256,8,256]{2,1,0:T(8,128)(2,1)} %bitcast.6), calls=%async_computation | async-start | bytes 2097152 | tf_op jit(solution)/shard_map/all_to_all | solution.py:179
  21.8 0.0 copy-done
  21.8 1.7 %mixing.1.mix_ref = f32[128,1024]{1,0:T(8,128)S(1)} custom-call(s32[8]{0:T(128)S(1)} %copy-done), custom_call_target="tpu_custom_call" | custom-call | tf_op jit(solution)/shard_map/mixing/pallas_call | solution.py:116
  23.5 0.0 copy-done.1
  23.5 0.1 reshape.36
  23.6 0.1 copy.9
  23.7 0.1 eq.15
  23.8 0.1 select_reduce_fusion.place_ref
  23.9 29.0 %all-to-all-done.rows_ref = bf16[256,8,256]{2,1,0:T(8,128)(2,1)S(1)} async-done(((bf16[256,8,256]{2,1,0:T(8,128)(2,1)}), bf16[256,8,256]{2,1,0:T(8,128)(2,1)S(1)}, u32[]{:S(2)}, u32[]{:S(2)}) %all-to-all-start) | async-done | bytes 1048608 | tf_op jit(solution)/shard_map/all_to_all | solution.py:179
  52.9 2.3 %mix.1 = bf16[2048,256]{1,0:T(8,128)(2,1)} custom-call(s32[256]{0:T(256)S(1)} %select_reduce_fusion.place_ref, f32[128,1024]{1,0:T(8,128)S(1)} %mixing.1.mix_ref, bf16[256,8,256]{2,1,0:T(8,128)(2,1)S(1)} %all-to-all-done.rows_ref), custom_call_target="tpu_custom_call" | custom-call | tf_op jit(solution)/shard_map/mix/pallas_call | solution.py:156
  55.2 6.4 %all-to-all-start.1 = ((bf16[256,8,256]{2,1,0:T(8,128)(2,1)}), bf16[256,8,256]{2,1,0:T(8,128)(2,1)S(1)}, u32[]{:S(2)}, u32[]{:S(2)}) async-start(bf16[256,8,256]{2,1,0:T(8,128)(2,1)} %bitcast.7), calls=%async_computation.1 | async-start | bytes 2097152 | tf_op jit(solution)/shard_map/all_to_all | solution.py:179
  61.7 5.2 %momentum_step.1 = bf16[32,16384]{1,0:T(8,128)(2,1)} custom-call(bf16[32,256]{1,0:T(8,128)(2,1)} %bitcast.26, bf16[256,16384]{1,0:T(8,128)(2,1)} %bitcast.17, bf16[256,16384]{1,0:T(8,128)(2,1)} %bitcast.18, bf16[32,16384]{1,0:T(8,128)(2,1)} %bitcast.21), custom_call_target="tpu_custom_call" | custom-call | tf_op jit(solution)/shard_map/momentum_step/pallas_call | solution.py:73
  66.8 25.9 %all-to-all-done.1 = bf16[256,8,256]{2,1,0:T(8,128)(2,1)S(1)} async-done(((bf16[256,8,256]{2,1,0:T(8,128)(2,1)}), bf16[256,8,256]{2,1,0:T(8,128)(2,1)S(1)}, u32[]{:S(2)}, u32[]{:S(2)}) %all-to-all-start.1) | async-done | bytes 1048608 | tf_op jit(solution)/shard_map/all_to_all | solution.py:179
  92.8 1.0 %copy.11 = bf16[1,1,1,32,16384]{4,3,2,1,0:T(8,128)(2,1)} copy(bf16[1,1,1,32,16384]{4,3,2,1,0:T(8,128)(2,1)S(1)} %bitcast.19) | data formatting | bytes 2097152
Async XLA Ops:
  0.6 21.2 %copy-start = (s32[8]{0:T(128)S(1)}, s32[8]{0:T(128)}, u32[]{:S(2)}) copy-start(s32[8]{0:T(128)} %shift_ref.1) | copy-start | bytes 100
  0.6 22.9 %copy-start.1 = (s32[256]{0:T(256)S(1)}, s32[256]{0:T(256)}, u32[]{:S(2)}) copy-start(s32[256]{0:T(256)} %param.10) | copy-start | bytes 3076
  6.2 46.7 %all-to-all-start = ((bf16[256,8,256]{2,1,0:T(8,128)(2,1)}), bf16[256,8,256]{2,1,0:T(8,128)(2,1)S(1)}, u32[]{:S(2)}, u32[]{:S(2)}) async-start(bf16[256,8,256]{2,1,0:T(8,128)(2,1)} %bitcast.6), calls=%async_computation | async-start | bytes 2097152 | tf_op jit(solution)/shard_map/all_to_all | solution.py:179
  55.2 37.5 %all-to-all-start.1 = ((bf16[256,8,256]{2,1,0:T(8,128)(2,1)}), bf16[256,8,256]{2,1,0:T(8,128)(2,1)S(1)}, u32[]{:S(2)}, u32[]{:S(2)}) async-start(bf16[256,8,256]{2,1,0:T(8,128)(2,1)} %bitcast.7), calls=%async_computation.1 | async-start | bytes 2097152 | tf_op jit(solution)/shard_map/all_to_all | solution.py:179

commit v2 on v1

--- a/solution.py
+++ b/solution.py
@@ -1,5 +1,3 @@
-import functools
-
 import jax
 import jax.numpy as jnp
 from jax import lax
@@ -86,49 +84,52 @@
     )(*in_hbm(grad_out, hidden, hidden, moment))
 
 
-def mixing_kernel(sizes, shift_ref, out_ref):
-    _, count_y, count_z = sizes
-    half = out_ref.shape[0]
+def mixing_kernel(shift_ref, out_ref):
+    wide = out_ref.shape[0]
+    half = wide // SUB
     row = lax.broadcasted_iota(jnp.int32, (half, half), 0)
     col = lax.broadcasted_iota(jnp.int32, (half, half), 1)
     gap = (row - col) & (half - 1)
-    place_x = row // (count_y * count_z)
-    place_z = row // count_y % count_z
-    place_y = row % count_y
-    mix = ((place_x * count_y + place_y) * count_z + place_z == col).astype(jnp.float32)
+    mix = (gap == 0).astype(jnp.float32)
     for step in range(shift_ref.shape[0]):
         offset = jnp.left_shift(jnp.int32(1), shift_ref[step]) & (half - 1)
         one = (gap == 0).astype(jnp.float32) + (gap == offset).astype(jnp.float32)
         mix = jnp.dot(
-            mix.astype(jnp.bfloat16), one.astype(jnp.bfloat16), preferred_element_type=jnp.float32
+            one.astype(jnp.bfloat16), mix.astype(jnp.bfloat16), preferred_element_type=jnp.float32
         )
-    wide = half * SUB
     spread_col = (
         lax.broadcasted_iota(jnp.int32, (half, wide), 1) // SUB
         == lax.broadcasted_iota(jnp.int32, (half, wide), 0)
     ).astype(jnp.bfloat16)
     wide_mix = jnp.dot(mix.astype(jnp.bfloat16), spread_col, preferred_element_type=jnp.float32)
-    out_ref[...] = wide_mix * (0.5 / half)
-
-
-def mixing(round_shift, sizes):
-    half = sizes[0] * sizes[1] * sizes[2] // 2
-    return pl.pallas_call(
-        functools.partial(mixing_kernel, sizes),
-        in_specs=[pl.BlockSpec(memory_space=pltpu.SMEM)],
-        out_specs=pl.BlockSpec(memory_space=pltpu.VMEM),
-        out_shape=pltpu.VMEM((half, half * SUB), jnp.float32),
-        compiler_params=pltpu.CompilerParams(vmem_limit_bytes=24 << 20),
-        name="mixing",
-    )(round_shift)
-
-
-def mix_kernel(place_ref, mix_ref, rows_ref, out_ref, full_ref, pair_ref):
-    half, wide = mix_ref.shape
+    wide_mix = wide_mix * (0.5 / half)
     same = (
         lax.broadcasted_iota(jnp.int32, (SUB, wide), 1) & (SUB - 1)
         == lax.broadcasted_iota(jnp.int32, (SUB, wide), 0)
     )
+    for at in range(0, half, 2):
+        lines = [
+            jnp.where(same, jnp.broadcast_to(wide_mix[k : k + 1], (SUB, wide)), 0.0)
+            for k in (at, at + 1)
+        ]
+        out_ref[at * SUB : (at + 2) * SUB] = jnp.concatenate(lines, axis=0).astype(jnp.bfloat16)
+
+
+def mixing(round_shift, workers):
+    wide = workers // 2 * SUB
+    return pl.pallas_call(
+        mixing_kernel,
+        in_specs=[pl.BlockSpec(memory_space=pltpu.SMEM)],
+        out_specs=pl.BlockSpec(memory_space=pltpu.VMEM),
+        out_shape=pltpu.VMEM((wide, wide), jnp.bfloat16),
+        compiler_params=pltpu.CompilerParams(vmem_limit_bytes=24 << 20),
+        name="mixing",
+    )(round_shift)
+
+
+def mix_kernel(place_ref, mix_ref, rows_ref, out_ref, pair_ref):
+    wide = mix_ref.shape[0]
+    half = wide // SUB
     for at in range(0, half, 2):
         pairs = [
             (
@@ -139,19 +140,14 @@
             for k in (at, at + 1)
         ]
         pair_ref[at * SUB : (at + 2) * SUB] = jnp.concatenate(pairs, axis=0).astype(jnp.bfloat16)
-        lines = [
-            jnp.where(same, jnp.broadcast_to(mix_ref[k : k + 1], (SUB, wide)), 0.0)
-            for k in (at, at + 1)
-        ]
-        full_ref[at * SUB : (at + 2) * SUB] = jnp.concatenate(lines, axis=0).astype(jnp.bfloat16)
-    mixed = jnp.dot(full_ref[...], pair_ref[...], preferred_element_type=jnp.float32)
+    mixed = jnp.dot(mix_ref[...], pair_ref[...], preferred_element_type=jnp.float32)
     mixed = mixed.astype(jnp.bfloat16)
     out_ref[:wide] = mixed
     out_ref[wide:] = mixed
 
 
 def mix(places, matrix, rows):
-    _, wide = matrix.shape
+    wide = matrix.shape[0]
     width = rows.shape[-1]
     return pl.pallas_call(
         mix_kernel,
@@ -162,10 +158,7 @@
         ],
         out_specs=pl.BlockSpec(memory_space=pltpu.VMEM),
         out_shape=pltpu.VMEM((2 * wide, width), jnp.bfloat16),
-        scratch_shapes=[
-            pltpu.VMEM((wide, wide), jnp.bfloat16),
-            pltpu.VMEM((wide, width), jnp.bfloat16),
-        ],
+        scratch_shapes=[pltpu.VMEM((wide, width), jnp.bfloat16)],
         compiler_params=pltpu.CompilerParams(vmem_limit_bytes=24 << 20),
         name="mix",
     )(
@@ -176,7 +169,7 @@
 
 
 def exchange(pieces):
-    return lax.all_to_all(pieces, ("gx", "gz", "gy"), split_axis=0, concat_axis=0, tiled=True)
+    return lax.all_to_all(pieces, ("gx", "gy", "gz"), split_axis=0, concat_axis=0, tiled=True)
 
 
 def shards(hidden_acts, output_grad, weights, momentum, worker_of_slot, round_shift):
@@ -190,10 +183,10 @@
     workers = count_x * count_y * count_z
     rows, _ = weight.shape
     groups = rows // SUB
-    held = worker_of_slot.reshape(count_z, count_y, count_x).transpose(2, 0, 1).reshape(1, workers)
+    held = worker_of_slot.reshape(count_z, count_y, count_x).transpose(2, 1, 0).reshape(1, workers)
     order = jnp.arange(workers, dtype=jnp.int32)
     places = jnp.sum(jnp.where(held == order[:, None], order[None, :], 0), axis=1, dtype=jnp.int32)
-    matrix = mixing(round_shift, (count_x, count_y, count_z))
+    matrix = mixing(round_shift, workers)
     pieces = local_step(grad_out, hidden, weight, moment, workers)
     received = exchange(pieces.reshape(workers, SUB, -1))
     new_moment = momentum_step(grad_out, hidden, moment)

time: 93.9 us -> 92.6 us (0.986)
  waiting for transfers between devices: 54.9 us -> 53.1 us
  local copies, waits for them, and re-layouts: 1.24 us -> 2.27 us
    all_to_all x2, waiting for transfers between devices: 54.9 us -> 53.1 us  [exchange(): lax.all_to_all(pieces, ('gx', 'gy', 'gz'), split_axis=0, concat_axis=0, t...]
    pallas_call x1, Pallas kernels: 2.32 us -> 1.34 us  [mix(): pl.pallas_call(mix_kernel, in_specs=[pl.BlockSpec(memory_space=pltpu.SMEM...]
    unnamed x5 -> x7, local copies, waits for them, and re-layouts: 0.98 us -> 1.94 us
  transfers between devices with their start and end apart: 2 -> 2, of which waited for: 2 -> 2; matrix products, arithmetic and copies ran while one was open for 0% -> 0% of each run, Pallas kernels for 7% -> 8%
where the time goes in v2:
time: 92.6 us; the launch traced here: 92.4 us
  waiting for transfers between devices  53.1 us (57%)
  starting transfers between devices  22.1 us (24%)
  Pallas kernels  14.1 us (15%)
  local copies, waits for them, and re-layouts  2.27 us (2%)
    all_to_all x2, waiting for transfers between devices, exchange(): lax.all_to_all(pieces, ('gx', 'gy', 'gz'), split_axis=0, concat_axis=0, t...  53.1 us
    all_to_all x2, starting transfers between devices, exchange(): lax.all_to_all(pieces, ('gx', 'gy', 'gz'), split_axis=0, concat_axis=0, t...  22.1 us
    pallas_call x1, Pallas kernels, local_step(): pl.pallas_call(step_kernel, grid=(cols // BLOCK,), in_specs=[pl.BlockSpec...  5.5 us
    pallas_call x1, Pallas kernels, momentum_step(): pl.pallas_call(moment_kernel, grid=(cols // BLOCK,), in_specs=[pl.BlockSp...  5.16 us
    pallas_call x1, Pallas kernels, mixing(): pl.pallas_call(mixing_kernel, in_specs=[pl.BlockSpec(memory_space=pltpu.S...  2.12 us
    unnamed x7, local copies, waits for them, and re-layouts  1.94 us
  transfers between devices with their start and end apart: 2, of which 2 were waited for; matrix products, arithmetic and copies ran while one was open for 0% of the time, Pallas kernels for 8%

profile of v2, /device:TPU:1, one launch (start us, length us, event | category | flops | bytes accessed | tf_op | source)
XLA Modules:
  0.0 92.4 jit_solution(6793541239595966899)
XLA Ops:
  0.6 0.0 copy-start.1
  0.6 0.0 copy-start.2
  0.7 5.5 %local_step.1 = bf16[4,64,8,256]{3,2,1,0:T(8,128)(2,1)} custom-call(bf16[32,256]{1,0:T(8,128)(2,1)} %bitcast.26, bf16[256,16384]{1,0:T(8,128)(2,1)} %bitcast.16, bf16[256,16384]{1,0:T(8,128)(2,1)} %bitcast.17, bf16[32,16384]{1,0:T(8,128)(2,1)} %bitcast.23, bf16[32,16384]{1,0:T(8,128)(2,1)} %bitcast.21), custom_call_target="tpu_custom_call" | custom-call | tf_op jit(solution)/shard_map/local_step/pallas_call | solution.py:50
  6.2 15.6 %all-to-all-start = ((bf16[256,8,256]{2,1,0:T(8,128)(2,1)}), bf16[256,8,256]{2,1,0:T(8,128)(2,1)S(1)}, u32[]{:S(2)}, u32[]{:S(2)}) async-start(bf16[256,8,256]{2,1,0:T(8,128)(2,1)} %bitcast.6), calls=%async_computation | async-start | bytes 2097152 | tf_op jit(solution)/shard_map/all_to_all | solution.py:172
  21.8 0.0 copy-done.1
  21.8 2.1 %mixing.1.mix_ref = bf16[1024,1024]{1,0:T(8,128)(2,1)S(1)} custom-call(s32[8]{0:T(128)S(1)} %copy-done.1), custom_call_target="tpu_custom_call" | custom-call | tf_op jit(solution)/shard_map/mixing/pallas_call | solution.py:120
  23.9 0.0 copy-done.2
  24.0 0.1 reshape.36
  24.0 0.1 copy.9
  24.2 0.1 eq.15
  24.3 0.1 select_reduce_fusion.place_ref
  24.4 28.0 %all-to-all-done.rows_ref = bf16[256,8,256]{2,1,0:T(8,128)(2,1)S(1)} async-done(((bf16[256,8,256]{2,1,0:T(8,128)(2,1)}), bf16[256,8,256]{2,1,0:T(8,128)(2,1)S(1)}, u32[]{:S(2)}, u32[]{:S(2)}) %all-to-all-start) | async-done | bytes 1048608 | tf_op jit(solution)/shard_map/all_to_all | solution.py:172
  52.4 1.3 %mix.1 = bf16[2048,256]{1,0:T(8,128)(2,1)S(1)} custom-call(s32[256]{0:T(256)S(1)} %select_reduce_fusion.place_ref, bf16[1024,1024]{1,0:T(8,128)(2,1)S(1)} %mixing.1.mix_ref, bf16[256,8,256]{2,1,0:T(8,128)(2,1)S(1)} %all-to-all-done.rows_ref), custom_call_target="tpu_custom_call" | custom-call | tf_op jit(solution)/shard_map/mix/pallas_call | solution.py:152
  53.7 0.0 copy-start
  53.7 1.0 %copy-done = bf16[2048,256]{1,0:T(8,128)(2,1)} copy-done((bf16[2048,256]{1,0:T(8,128)(2,1)}, bf16[2048,256]{1,0:T(8,128)(2,1)S(1)}, u32[]{:S(2)}) %copy-start) | copy-done | bytes 1048600
  54.7 6.4 %all-to-all-start.1 = ((bf16[256,8,256]{2,1,0:T(8,128)(2,1)}), bf16[256,8,256]{2,1,0:T(8,128)(2,1)S(1)}, u32[]{:S(2)}, u32[]{:S(2)}) async-start(bf16[256,8,256]{2,1,0:T(8,128)(2,1)} %bitcast.15), calls=%async_computation.1 | async-start | bytes 2097152 | tf_op jit(solution)/shard_map/all_to_all | solution.py:172
  61.1 5.2 %momentum_step.1 = bf16[32,16384]{1,0:T(8,128)(2,1)} custom-call(bf16[32,256]{1,0:T(8,128)(2,1)} %bitcast.27, bf16[256,16384]{1,0:T(8,128)(2,1)} %bitcast.18, bf16[256,16384]{1,0:T(8,128)(2,1)} %bitcast.19, bf16[32,16384]{1,0:T(8,128)(2,1)} %bitcast.22), custom_call_target="tpu_custom_call" | custom-call | tf_op jit(solution)/shard_map/momentum_step/pallas_call | solution.py:71
  66.3 25.1 %all-to-all-done.1 = bf16[256,8,256]{2,1,0:T(8,128)(2,1)S(1)} async-done(((bf16[256,8,256]{2,1,0:T(8,128)(2,1)}), bf16[256,8,256]{2,1,0:T(8,128)(2,1)S(1)}, u32[]{:S(2)}, u32[]{:S(2)}) %all-to-all-start.1) | async-done | bytes 1048608 | tf_op jit(solution)/shard_map/all_to_all | solution.py:172
  91.4 1.0 %copy.11 = bf16[1,1,1,32,16384]{4,3,2,1,0:T(8,128)(2,1)} copy(bf16[1,1,1,32,16384]{4,3,2,1,0:T(8,128)(2,1)S(1)} %bitcast.20) | data formatting | bytes 2097152
Async XLA Ops:
  0.6 21.2 %copy-start.1 = (s32[8]{0:T(128)S(1)}, s32[8]{0:T(128)}, u32[]{:S(2)}) copy-start(s32[8]{0:T(128)} %shift_ref.1) | copy-start | bytes 100
  0.6 23.3 %copy-start.2 = (s32[256]{0:T(256)S(1)}, s32[256]{0:T(256)}, u32[]{:S(2)}) copy-start(s32[256]{0:T(256)} %param.10) | copy-start | bytes 3076
  6.2 46.2 %all-to-all-start = ((bf16[256,8,256]{2,1,0:T(8,128)(2,1)}), bf16[256,8,256]{2,1,0:T(8,128)(2,1)S(1)}, u32[]{:S(2)}, u32[]{:S(2)}) async-start(bf16[256,8,256]{2,1,0:T(8,128)(2,1)} %bitcast.6), calls=%async_computation | async-start | bytes 2097152 | tf_op jit(solution)/shard_map/all_to_all | solution.py:172
  53.7 1.0 %copy-start = (bf16[2048,256]{1,0:T(8,128)(2,1)}, bf16[2048,256]{1,0:T(8,128)(2,1)S(1)}, u32[]{:S(2)}) copy-start(bf16[2048,256]{1,0:T(8,128)(2,1)S(1)} %mix.1) | copy-start | bytes 3145732
  54.7 36.7 %all-to-all-start.1 = ((bf16[256,8,256]{2,1,0:T(8,128)(2,1)}), bf16[256,8,256]{2,1,0:T(8,128)(2,1)S(1)}, u32[]{:S(2)}, u32[]{:S(2)}) async-start(bf16[256,8,256]{2,1,0:T(8,128)(2,1)} %bitcast.15), calls=%async_computation.1 | async-start | bytes 2097152 | tf_op jit(solution)/shard_map/all_to_all | solution.py:172

commit v3 on v2

--- a/solution.py
+++ b/solution.py
@@ -102,7 +102,7 @@
         == lax.broadcasted_iota(jnp.int32, (half, wide), 0)
     ).astype(jnp.bfloat16)
     wide_mix = jnp.dot(mix.astype(jnp.bfloat16), spread_col, preferred_element_type=jnp.float32)
-    wide_mix = wide_mix * (0.5 / half)
+    wide_mix = wide_mix * (0.25 / half)
     same = (
         lax.broadcasted_iota(jnp.int32, (SUB, wide), 1) & (SUB - 1)
         == lax.broadcasted_iota(jnp.int32, (SUB, wide), 0)
@@ -131,15 +131,8 @@
     wide = mix_ref.shape[0]
     half = wide // SUB
     for at in range(0, half, 2):
-        pairs = [
-            (
-                rows_ref[place_ref[k]].astype(jnp.float32)
-                + rows_ref[place_ref[k + half]].astype(jnp.float32)
-            )
-            * 0.5
-            for k in (at, at + 1)
-        ]
-        pair_ref[at * SUB : (at + 2) * SUB] = jnp.concatenate(pairs, axis=0).astype(jnp.bfloat16)
+        pairs = [rows_ref[place_ref[k]] + rows_ref[place_ref[k + half]] for k in (at, at + 1)]
+        pair_ref[at * SUB : (at + 2) * SUB] = jnp.concatenate(pairs, axis=0)
     mixed = jnp.dot(mix_ref[...], pair_ref[...], preferred_element_type=jnp.float32)
     mixed = mixed.astype(jnp.bfloat16)
     out_ref[:wide] = mixed

time: 92.6 us -> 92.6 us (level)
  no operation moved by 1% of the time
where the time goes in v3:
time: 92.6 us; the launch traced here: 92.4 us
  waiting for transfers between devices  53.1 us (57%)
  starting transfers between devices  22.1 us (24%)
  Pallas kernels  14.1 us (15%)
  local copies, waits for them, and re-layouts  2.27 us (2%)
    all_to_all x2, waiting for transfers between devices, exchange(): lax.all_to_all(pieces, ('gx', 'gy', 'gz'), split_axis=0, concat_axis=0, t...  53.1 us
    all_to_all x2, starting transfers between devices, exchange(): lax.all_to_all(pieces, ('gx', 'gy', 'gz'), split_axis=0, concat_axis=0, t...  22.1 us
    pallas_call x1, Pallas kernels, local_step(): pl.pallas_call(step_kernel, grid=(cols // BLOCK,), in_specs=[pl.BlockSpec...  5.5 us
    pallas_call x1, Pallas kernels, momentum_step(): pl.pallas_call(moment_kernel, grid=(cols // BLOCK,), in_specs=[pl.BlockSp...  5.16 us
    pallas_call x1, Pallas kernels, mixing(): pl.pallas_call(mixing_kernel, in_specs=[pl.BlockSpec(memory_space=pltpu.S...  2.12 us
    unnamed x7, local copies, waits for them, and re-layouts  1.94 us
  transfers between devices with their start and end apart: 2, of which 2 were waited for; matrix products, arithmetic and copies ran while one was open for 0% of the time, Pallas kernels for 8%

profile of v3, /device:TPU:1, one launch (start us, length us, event | category | flops | bytes accessed | tf_op | source)
XLA Modules:
  0.0 92.4 jit_solution(12430397099275917686)
XLA Ops:
  0.6 0.0 copy-start.1
  0.6 0.0 copy-start.2
  0.7 5.5 %local_step.1 = bf16[4,64,8,256]{3,2,1,0:T(8,128)(2,1)} custom-call(bf16[32,256]{1,0:T(8,128)(2,1)} %bitcast.26, bf16[256,16384]{1,0:T(8,128)(2,1)} %bitcast.16, bf16[256,16384]{1,0:T(8,128)(2,1)} %bitcast.17, bf16[32,16384]{1,0:T(8,128)(2,1)} %bitcast.23, bf16[32,16384]{1,0:T(8,128)(2,1)} %bitcast.21), custom_call_target="tpu_custom_call" | custom-call | tf_op jit(solution)/shard_map/local_step/pallas_call | solution.py:50
  6.2 15.6 %all-to-all-start = ((bf16[256,8,256]{2,1,0:T(8,128)(2,1)}), bf16[256,8,256]{2,1,0:T(8,128)(2,1)S(1)}, u32[]{:S(2)}, u32[]{:S(2)}) async-start(bf16[256,8,256]{2,1,0:T(8,128)(2,1)} %bitcast.6), calls=%async_computation | async-start | bytes 2097152 | tf_op jit(solution)/shard_map/all_to_all | solution.py:165
  21.8 0.0 copy-done.1
  21.8 2.1 %mixing.1.mix_ref = bf16[1024,1024]{1,0:T(8,128)(2,1)S(1)} custom-call(s32[8]{0:T(128)S(1)} %copy-done.1), custom_call_target="tpu_custom_call" | custom-call | tf_op jit(solution)/shard_map/mixing/pallas_call | solution.py:120
  23.9 0.0 copy-done.2
  24.0 0.1 reshape.36
  24.0 0.1 copy.9
  24.2 0.1 eq.15
  24.3 0.1 select_reduce_fusion.place_ref
  24.4 28.0 %all-to-all-done.rows_ref = bf16[256,8,256]{2,1,0:T(8,128)(2,1)S(1)} async-done(((bf16[256,8,256]{2,1,0:T(8,128)(2,1)}), bf16[256,8,256]{2,1,0:T(8,128)(2,1)S(1)}, u32[]{:S(2)}, u32[]{:S(2)}) %all-to-all-start) | async-done | bytes 1048608 | tf_op jit(solution)/shard_map/all_to_all | solution.py:165
  52.4 1.3 %mix.1 = bf16[2048,256]{1,0:T(8,128)(2,1)S(1)} custom-call(s32[256]{0:T(256)S(1)} %select_reduce_fusion.place_ref, bf16[1024,1024]{1,0:T(8,128)(2,1)S(1)} %mixing.1.mix_ref, bf16[256,8,256]{2,1,0:T(8,128)(2,1)S(1)} %all-to-all-done.rows_ref), custom_call_target="tpu_custom_call" | custom-call | tf_op jit(solution)/shard_map/mix/pallas_call | solution.py:145
  53.7 0.0 copy-start
  53.7 1.0 %copy-done = bf16[2048,256]{1,0:T(8,128)(2,1)} copy-done((bf16[2048,256]{1,0:T(8,128)(2,1)}, bf16[2048,256]{1,0:T(8,128)(2,1)S(1)}, u32[]{:S(2)}) %copy-start) | copy-done | bytes 1048600
  54.7 6.4 %all-to-all-start.1 = ((bf16[256,8,256]{2,1,0:T(8,128)(2,1)}), bf16[256,8,256]{2,1,0:T(8,128)(2,1)S(1)}, u32[]{:S(2)}, u32[]{:S(2)}) async-start(bf16[256,8,256]{2,1,0:T(8,128)(2,1)} %bitcast.15), calls=%async_computation.1 | async-start | bytes 2097152 | tf_op jit(solution)/shard_map/all_to_all | solution.py:165
  61.1 5.2 %momentum_step.1 = bf16[32,16384]{1,0:T(8,128)(2,1)} custom-call(bf16[32,256]{1,0:T(8,128)(2,1)} %bitcast.27, bf16[256,16384]{1,0:T(8,128)(2,1)} %bitcast.18, bf16[256,16384]{1,0:T(8,128)(2,1)} %bitcast.19, bf16[32,16384]{1,0:T(8,128)(2,1)} %bitcast.22), custom_call_target="tpu_custom_call" | custom-call | tf_op jit(solution)/shard_map/momentum_step/pallas_call | solution.py:71
  66.3 25.1 %all-to-all-done.1 = bf16[256,8,256]{2,1,0:T(8,128)(2,1)S(1)} async-done(((bf16[256,8,256]{2,1,0:T(8,128)(2,1)}), bf16[256,8,256]{2,1,0:T(8,128)(2,1)S(1)}, u32[]{:S(2)}, u32[]{:S(2)}) %all-to-all-start.1) | async-done | bytes 1048608 | tf_op jit(solution)/shard_map/all_to_all | solution.py:165
  91.4 1.0 %copy.11 = bf16[1,1,1,32,16384]{4,3,2,1,0:T(8,128)(2,1)} copy(bf16[1,1,1,32,16384]{4,3,2,1,0:T(8,128)(2,1)S(1)} %bitcast.20) | data formatting | bytes 2097152
Async XLA Ops:
  0.6 21.2 %copy-start.1 = (s32[8]{0:T(128)S(1)}, s32[8]{0:T(128)}, u32[]{:S(2)}) copy-start(s32[8]{0:T(128)} %shift_ref.1) | copy-start | bytes 100
  0.6 23.3 %copy-start.2 = (s32[256]{0:T(256)S(1)}, s32[256]{0:T(256)}, u32[]{:S(2)}) copy-start(s32[256]{0:T(256)} %param.10) | copy-start | bytes 3076
  6.2 46.2 %all-to-all-start = ((bf16[256,8,256]{2,1,0:T(8,128)(2,1)}), bf16[256,8,256]{2,1,0:T(8,128)(2,1)S(1)}, u32[]{:S(2)}, u32[]{:S(2)}) async-start(bf16[256,8,256]{2,1,0:T(8,128)(2,1)} %bitcast.6), calls=%async_computation | async-start | bytes 2097152 | tf_op jit(solution)/shard_map/all_to_all | solution.py:165
  53.7 1.0 %copy-start = (bf16[2048,256]{1,0:T(8,128)(2,1)}, bf16[2048,256]{1,0:T(8,128)(2,1)S(1)}, u32[]{:S(2)}) copy-start(bf16[2048,256]{1,0:T(8,128)(2,1)S(1)} %mix.1) | copy-start | bytes 3145732
  54.7 36.7 %all-to-all-start.1 = ((bf16[256,8,256]{2,1,0:T(8,128)(2,1)}), bf16[256,8,256]{2,1,0:T(8,128)(2,1)S(1)}, u32[]{:S(2)}, u32[]{:S(2)}) async-start(bf16[256,8,256]{2,1,0:T(8,128)(2,1)} %bitcast.15), calls=%async_computation.1 | async-start | bytes 2097152 | tf_op jit(solution)/shard_map/all_to_all | solution.py:165
